TPU v7x, 32 devices: a whole 2x2x4 slice. The times are simulated.
32 devices in a mesh: segment: 4 (over y, x), amp: 8 (over z, core).
Axes of the slice: x: 2, y: 2, z: 4, core: 2. Of those that a mesh axis runs over, the one named last changes fastest.
Arguments:
- states: float32 [4, 2097152], P('segment', 'amp'), may hold values from -6 to 6
- gate_blocks: float32 [4, 3, 128, 128], P('segment'), may hold values from -1 to 1, as said below
- kraus_picks: int32 [4, 4, 3, 7], P('segment'), may hold values from 0 to 3
- block_targets: int32 [4, 3], replicated, may hold values from 0 to 1
Outputs:
- final_states: float32 [4, 2097152], P('segment', 'amp')
- log_weights: float32 [4, 4], P('segment')
Inputs may be any that keep to these rules, and one draw needn't show every extreme that they name: Every block of gate_blocks is an orthogonal matrix, up to rounding.
All inputs are finite; a program needn't handle non-finite values.
Results may differ from a plain program's by a relative error of at most 0.0003.
Values sent between devices are 32-bit elements; how exact they have to be, the bound alone decides.
A program may use at most 64 MiB of HBM per device.

v0:
```python
import functools

import jax
import jax.numpy as jnp
from jax import lax
from jax.experimental import pallas as pl
from jax.experimental.pallas import tpu as pltpu
from jax.sharding import PartitionSpec as P

KEEP_FACTORS = (1.0, 0.9, 1.0, 0.97)
FLIP_FACTORS = (0.9, 1.0, 0.97, 1.0)
MESH = pl.DeviceIdType.MESH


def broadcast(block, axis, owner):
    block = jnp.where(lax.axis_index(axis) == owner, block, jnp.zeros_like(block))
    return lax.psum(block, axis)


def noise_factors(kraus_rows):
    qubit_count = kraus_rows.shape[-1]
    register = 2**qubit_count
    positions = jnp.arange(register, dtype=jnp.int32)
    product = jnp.ones(kraus_rows.shape[:-1] + (register,), jnp.float32)
    for qubit_pos in range(qubit_count):
        bit_value = jnp.right_shift(positions, qubit_count - 1 - qubit_pos) & 1
        column = kraus_rows[..., qubit_pos : qubit_pos + 1]
        low_value = jnp.zeros(column.shape, jnp.float32)
        high_value = jnp.zeros(column.shape, jnp.float32)
        for option in range(4):
            picked = (column == option).astype(jnp.float32)
            low_value = low_value + picked * KEEP_FACTORS[option]
            high_value = high_value + picked * FLIP_FACTORS[option]
        product = product * jnp.where(bit_value == 1, high_value, low_value)
    return product


def apply_gate(amplitudes, matrix, factors, target):

    def on_low(values):
        mixed_rows = jnp.einsum("bhmk,ik->bhmi", values, matrix, precision=lax.Precision.HIGHEST)
        return mixed_rows * factors[:, None, None, :]

    def on_high(values):
        mixed_rows = jnp.einsum("bjmk,ij->bimk", values, matrix, precision=lax.Precision.HIGHEST)
        return mixed_rows * factors[:, :, None, None]

    return lax.cond(target == 0, on_low, on_high, amplitudes)


def square_sums(values):
    return (values, jnp.sum(values * values, axis=(1, 2, 3)))


def body(states, gate_blocks, kraus_picks, block_targets):
    traj_here = states.shape[0]
    amp_local = states.shape[1]
    register = gate_blocks.shape[-1]
    blocks = gate_blocks.shape[1]
    middle = amp_local // (register * register)
    total_amps = amp_local * lax.axis_size("amp")
    sections = lax.axis_size("segment")
    amplitudes = states.reshape(traj_here, register, middle, register)
    first_local = jnp.sum(amplitudes * amplitudes, axis=(1, 2, 3))
    local_sums = [first_local]
    for section in range(sections):
        section_gates = broadcast(gate_blocks, "segment", section)[0]
        for block_pos in range(blocks):
            factors = noise_factors(kraus_picks[:, section, block_pos, :])
            amplitudes = apply_gate(
                amplitudes, section_gates[block_pos], factors, block_targets[section, block_pos]
            )
        amplitudes, local_sq = square_sums(
            lax.all_to_all(amplitudes, "amp", split_axis=1, concat_axis=1, tiled=True)
        )
        local_sums.append(local_sq)
    totals = lax.psum(jnp.stack(local_sums, axis=1), "amp")
    log_weights = jnp.log(totals[:, 1:] / totals[:, :-1])
    amplitudes = amplitudes / jnp.sqrt(totals[:, -1] / total_amps)[:, None, None, None]
    return (amplitudes.reshape(traj_here, amp_local), log_weights)


def partner(index, k):
    result = index
    bit = 1
    while bit <= k:
        if k & bit:
            result = result + bit * (1 - 2 * ((index // bit) % 2))
        bit *= 2
    return result


def split(values):
    high = values.astype(jnp.bfloat16)
    low = (values - high.astype(jnp.float32)).astype(jnp.bfloat16)
    return high, low


def left_form(matrix):
    return jnp.concatenate(split(matrix), axis=1)


def right_form(matrix):
    row = jnp.concatenate(split(matrix), axis=1)
    return jnp.concatenate([row, row], axis=0)


def multiply(left, right):
    both = jnp.dot(left, right, preferred_element_type=jnp.float32)
    half = both.shape[1] // 2
    return both[:, :half] + both[:, half:]


def fold_rows(values):
    squares = values * values
    return jnp.sum(squares.reshape(-1, 8, squares.shape[-1]), axis=0)


def row_factors(picks_ref, section, block, qubits, shape):
    positions = lax.broadcasted_iota(jnp.int32, shape, 0)
    product = jnp.ones(shape, jnp.float32)
    for q in range(qubits):
        pick = picks_ref[0, block, section, q]
        keep = jnp.float32(KEEP_FACTORS[0])
        flip = jnp.float32(FLIP_FACTORS[0])
        for option in range(1, 4):
            keep = jnp.where(pick == option, jnp.float32(KEEP_FACTORS[option]), keep)
            flip = jnp.where(pick == option, jnp.float32(FLIP_FACTORS[option]), flip)
        bit = jnp.right_shift(positions, qubits - 1 - q) & 1
        product = product * jnp.where(bit == 1, flip, keep)
    return product


def circuit_kernel(
    peers, sections, blocks, qubits, chunks, total_amps,
    x_hbm, gates_hbm, picks_ref, targets_ref,
    out_ref, logs_ref,
    xs, yin, ov, gates, low_form, high_form, partial, sums,
    x_sem, own_sem, gate_sem, gsend, grecv, isend, irecv, osend, orecv, ssend, srecv,
    entered,
):
    seg = lax.axis_index("segment")
    amp = lax.axis_index("amp")
    reg = gates.shape[-1]
    middle = chunks * peers
    order = list(range(peers - 1, 0, -1))

    loads = []
    for chunk in range(chunks):
        for d in range(peers):
            m = chunk * peers + d
            load = pltpu.make_async_copy(x_hbm.at[:, m, 0], xs.at[m], x_sem.at[m])
            load.start()
            loads.append(load)
    gate_load = pltpu.make_async_copy(gates_hbm, gates.at[seg], gate_sem)
    gate_load.start()
    own_loads = []
    for chunk in range(chunks):
        own = pltpu.make_async_copy(
            x_hbm.at[:, chunk * peers + amp, 0], yin.at[chunk, amp], own_sem.at[chunk]
        )
        own.start()
        own_loads.append(own)

    in_copies = []
    for chunk in range(chunks):
        copies = {}
        for k in order:
            peer = partner(amp, k)
            copies[k] = pltpu.make_async_remote_copy(
                src_ref=xs.at[chunk * peers + peer],
                dst_ref=yin.at[chunk, amp],
                send_sem=isend.at[chunk, k],
                recv_sem=irecv.at[chunk, k],
                device_id={"amp": peer},
                device_id_type=MESH,
            )
        in_copies.append(copies)

    def tell(semaphore, axis, index, k):
        pl.semaphore_signal(
            semaphore, inc=1, device_id={axis: partner(index, k)}, device_id_type=MESH
        )

    barrier = pltpu.get_barrier_semaphore()
    if peers == 8 and sections == 4:
        pair_at = amp // 2
        inner_pair = (pair_at + 1) // 2 % 2
        is_inner = inner_pair == 1
        for k in (1, 2):
            tell(barrier, "segment", seg, k)
        for k in (1, 2, 3):
            tell(barrier, "amp", amp, k)

        @pl.when(is_inner)
        def _():
            tell(barrier, "amp", amp, 6)
            tell(barrier, "amp", amp, 7)

        for load in loads:
            load.wait()
        pl.semaphore_wait(barrier, 5 + 2 * inner_pair)

        @pl.when(is_inner)
        def _():
            tell(entered.at[0], "amp", amp, 2)
            tell(entered.at[0], "amp", amp, 6)
            in_copies[0][6].start()
            in_copies[0][7].start()

        tell(entered.at[2], "segment", seg, 1)
        pl.semaphore_wait(entered.at[0], 1)

        @pl.when(is_inner)
        def _():
            tell(entered.at[1], "amp", amp, 2)

        in_copies[0][4].start()
        in_copies[0][5].start()

        @pl.when(jnp.logical_not(is_inner))
        def _():
            pl.semaphore_wait(entered.at[1], 1)
            in_copies[0][6].start()
            in_copies[0][7].start()

        for k in (3, 2, 1):
            in_copies[0][k].start()
        rest = in_copies[1:]
        pl.semaphore_wait(entered.at[2], 1)
    else:
        for k in order:
            tell(barrier, "amp", amp, k)
        for k in range(1, sections):
            tell(barrier, "segment", seg, k)
        for load in loads:
            load.wait()
        pl.semaphore_wait(barrier, peers - 1 + sections - 1)
        rest = in_copies
    for copies in rest:
        for k in order:
            copies[k].start()
    in_copies = [list(copies.values()) for copies in in_copies]

    gate_load.wait()
    gate_copies = []
    for k in range(1, sections):
        copy = pltpu.make_async_remote_copy(
            src_ref=gates.at[seg],
            dst_ref=gates.at[seg],
            send_sem=gsend.at[k],
            recv_sem=grecv.at[k],
            device_id={"segment": partner(seg, k)},
            device_id_type=MESH,
        )
        copy.start()
        gate_copies.append(copy)
    for copy in gate_copies:
        copy.wait_recv()

    rows_at = lax.broadcasted_iota(jnp.int32, (reg, reg), 0)
    columns_at = lax.broadcasted_iota(jnp.int32, (reg, reg), 1)
    identity = jnp.where(rows_at == columns_at, jnp.float32(1.0), jnp.float32(0.0))

    def build(section, carry):
        low = high = None
        for b in range(blocks):
            factors = row_factors(picks_ref, section, b, qubits, (reg, reg))
            damped = gates[section, b] * factors
            is_low = targets_ref[section, b] == 0
            for_low = jnp.where(is_low, damped, identity)
            for_high = jnp.where(is_low, identity, damped)
            if b == 0:
                low, high = for_low, for_high
            else:
                low = multiply(left_form(for_low), right_form(low))
                high = multiply(left_form(for_high), right_form(high))
        low_form[section] = right_form(low.T)
        high_form[section] = left_form(high)
        return carry

    lax.fori_loop(0, sections, build, 0)

    inner = reg // peers
    partial[...] = jnp.zeros_like(partial)

    def apply_section(chunk, section, swapped):
        low = low_form[section]
        high = high_form[section]
        total = jnp.zeros((8, reg), jnp.float32)
        for slab in range(peers):
            if swapped:
                value = yin[chunk, :, slab * inner : (slab + 1) * inner, :].reshape(reg, reg)
            else:
                value = yin[chunk, slab]
            value = multiply(left_form(value), low)
            value = multiply(high, right_form(value))
            total = total + fold_rows(value)
            if swapped:
                yin[chunk, :, slab * inner : (slab + 1) * inner, :] = value.reshape(
                    peers, inner, reg
                )
            else:
                yin[chunk, slab] = value
        partial[section + 1] = partial[section + 1] + total

    out_copies = []
    order_out = [5, 4, 7, 6, 3, 2, 1]
    for chunk in range(chunks):
        own_loads[chunk].wait()
        for copy in in_copies[chunk]:
            copy.wait_recv()
        first = jnp.zeros((8, reg), jnp.float32)
        for slab in range(peers):
            first = first + fold_rows(yin[chunk, slab])
        partial[0] = partial[0] + first

        def pair(i, carry, chunk=chunk):
            apply_section(chunk, 2 * i, False)
            apply_section(chunk, 2 * i + 1, True)
            return carry

        lax.fori_loop(0, sections // 2, pair, 0)

        if chunk == chunks - 1:
            for s in range(sections + 1):
                sums[amp, s : s + 1, :] = jnp.sum(partial[s], axis=0, keepdims=True)
            sum_copies = []
            for k in order:
                copy = pltpu.make_async_remote_copy(
                    src_ref=sums.at[amp],
                    dst_ref=sums.at[amp],
                    send_sem=ssend.at[k],
                    recv_sem=srecv.at[k],
                    device_id={"amp": partner(amp, k)},
                    device_id_type=MESH,
                )
                copy.start()
                sum_copies.append(copy)
        copies = []
        for k in order_out:
            peer = partner(amp, k)
            copy = pltpu.make_async_remote_copy(
                src_ref=yin.at[chunk, peer],
                dst_ref=ov.at[chunk, amp],
                send_sem=osend.at[chunk, k],
                recv_sem=orecv.at[chunk, k],
                device_id={"amp": peer},
                device_id_type=MESH,
            )
            copy.start()
            copies.append(copy)
        out_copies.append(copies)

    for copy in sum_copies:
        copy.wait_recv()
    totals = []
    for s in range(sections + 1):
        total = sums[0, s : s + 1, :]
        for d in range(1, peers):
            total = total + sums[d, s : s + 1, :]
        totals.append(jnp.sum(total, axis=1, keepdims=True))
    lanes = lax.broadcasted_iota(jnp.int32, (1, reg), 1)
    logs = jnp.zeros((1, reg), jnp.float32)
    for s in range(sections):
        logs = jnp.where(lanes == s, jnp.log(totals[s + 1] / totals[s]), logs)
    logs_ref[...] = logs[:, :sections]
    scale = 1.0 / jnp.sqrt(totals[sections] / total_amps)
    scale = jnp.broadcast_to(scale, (1, reg))

    for chunk in range(chunks):
        m = chunk * peers + amp
        out_ref[pl.ds(m, reg, stride=middle), :] = yin[chunk, amp] * scale
    for chunk in range(chunks):
        for at, k in reversed(list(enumerate(order_out))):
            out_copies[chunk][at].wait_recv()
            m = chunk * peers + partner(amp, k)
            out_ref[pl.ds(m, reg, stride=middle), :] = ov[chunk, partner(amp, k)] * scale

    for copies in in_copies + out_copies + [gate_copies, sum_copies]:
        for copy in copies:
            copy.wait_send()


def step(states, gate_blocks, kraus_picks, block_targets):
    traj_here, amp_local = states.shape
    reg = gate_blocks.shape[-1]
    blocks = gate_blocks.shape[1]
    qubits = kraus_picks.shape[-1]
    peers = lax.axis_size("amp")
    sections = lax.axis_size("segment")
    middle = amp_local // (reg * reg)
    fits = (
        traj_here == 1
        and gate_blocks.shape[0] == 1
        and middle % peers == 0
        and peers & (peers - 1) == 0
        and sections & (sections - 1) == 0
        and sections % 2 == 0
        and sections < 8
        and reg == 128
        and reg % (8 * peers) == 0
    )
    if not fits:
        return body(states, gate_blocks, kraus_picks, block_targets)
    chunks = middle // peers
    kernel = functools.partial(
        circuit_kernel, peers, sections, blocks, qubits, chunks, amp_local * peers
    )
    f32 = jnp.float32
    dma = pltpu.SemaphoreType.DMA
    out, logs = pl.pallas_call(
        kernel,
        out_shape=(
            pltpu.VMEM((reg * middle, reg), f32),
            pltpu.VMEM((1, sections), f32),
        ),
        in_specs=[
            pl.BlockSpec(memory_space=pl.ANY),
            pl.BlockSpec(memory_space=pl.ANY),
            pl.BlockSpec(memory_space=pltpu.SMEM),
            pl.BlockSpec(memory_space=pltpu.SMEM),
        ],
        out_specs=(
            pl.BlockSpec(memory_space=pltpu.VMEM),
            pl.BlockSpec(memory_space=pltpu.VMEM),
        ),
        scratch_shapes=[
            pltpu.VMEM((middle, reg, reg), f32),
            pltpu.VMEM((chunks, peers, reg, reg), f32),
            pltpu.VMEM((chunks, peers, reg, reg), f32),
            pltpu.VMEM((sections, blocks, reg, reg), f32),
            pltpu.VMEM((sections, 2 * reg, 2 * reg), jnp.bfloat16),
            pltpu.VMEM((sections, reg, 2 * reg), jnp.bfloat16),
            pltpu.VMEM((sections + 1, 8, reg), f32),
            pltpu.VMEM((peers, 8, reg), f32),
            dma((middle,)),
            dma((chunks,)),
            dma,
            dma((sections,)),
            dma((sections,)),
            dma((chunks, peers)),
            dma((chunks, peers)),
            dma((chunks, peers)),
            dma((chunks, peers)),
            dma((peers,)),
            dma((peers,)),
            pltpu.SemaphoreType.REGULAR((3,)),
        ],
        compiler_params=pltpu.CompilerParams(collective_id=0, has_side_effects=True),
    )(
        states.reshape(reg, middle, 1, reg),
        gate_blocks[0],
        jnp.swapaxes(kraus_picks, 1, 2),
        block_targets,
    )
    return out.reshape(1, amp_local), logs


def solution(mesh):
    in_specs = (
        P("segment", "amp"),
        P("segment", None, None, None),
        P("segment", None, None, None),
        P(),
    )
    out_specs = (P("segment", "amp"), P("segment", None))
    return jax.shard_map(step, mesh=mesh, in_specs=in_specs, out_specs=out_specs, check_vma=False)
```

profile of v0, /device:TPU:9, one launch (start us, length us, event | category | flops | bytes accessed | tf_op | source)
XLA Modules:
  0.0 53.7 jit_solution(8490598166374869127)
XLA Ops:
  0.6 51.6 %shard_map.59 = (f32[2048,128]{1,0:T(8,128)S(1)}, f32[1,4]{1,0:T(1,128)S(1)}) custom-call(f32[128,16,1,128]{3,2,1,0:T(1,128)} %bitcast.5, f32[3,128,128]{2,1,0:T(8,128)} %bitcast.6, s32[1,3,4,7]{3,2,1,0:T(4,128)} %bitcast.7, s32[4,3]{1,0:T(4,128)} %targets_ref.1), custom_call_target="tpu_custom_call" | custom-call | tf_op jit(solution)/shard_map/pallas_call | solution.py:412
  52.3 1.0 %copy.8 = f32[1,262144]{1,0:T(1,128)} copy(f32[1,262144]{1,0:T(1,128)S(1)} %bitcast.4) | data formatting | bytes 2097152
  53.2 0.5 copy.9
where the time goes:
time: 54.4 us; the launch traced here: 53.7 us
  Pallas kernels  51.6 us (95%)
  local copies, waits for them, and re-layouts  1.48 us (3%)
  between operations  0.64 us (1%)
    pallas_call x1, Pallas kernels, step(): pl.pallas_call(kernel, out_shape=(pltpu.VMEM((reg * middle, reg), f32), p...  51.6 us
    unnamed x2, local copies, waits for them, and re-layouts  1.48 us

commit v1 on v0

--- a/solution.py
+++ b/solution.py
@@ -131,51 +131,26 @@
     return product
 
 
+def waits(like, semaphore):
+    pltpu.make_async_copy(like, like, semaphore).wait()
+
+
 def circuit_kernel(
     peers, sections, blocks, qubits, chunks, total_amps,
-    x_hbm, gates_hbm, picks_ref, targets_ref,
+    x_hbm, gates_hbm, picks_hbm, targets_hbm,
     out_ref, logs_ref,
-    xs, yin, ov, gates, low_form, high_form, partial, sums,
-    x_sem, own_sem, gate_sem, gsend, grecv, isend, irecv, osend, orecv, ssend, srecv,
+    xs, yin, ov, gates, picks, targets, low_form, high_form, partial, sums,
+    x_sem, own_sem, gate_sem, small_sem, gsend, grecv, isend, irecv, osend, orecv, ssend, srecv,
     entered,
 ):
     seg = lax.axis_index("segment")
     amp = lax.axis_index("amp")
     reg = gates.shape[-1]
     middle = chunks * peers
-    order = list(range(peers - 1, 0, -1))
-
-    loads = []
-    for chunk in range(chunks):
-        for d in range(peers):
-            m = chunk * peers + d
-            load = pltpu.make_async_copy(x_hbm.at[:, m, 0], xs.at[m], x_sem.at[m])
-            load.start()
-            loads.append(load)
-    gate_load = pltpu.make_async_copy(gates_hbm, gates.at[seg], gate_sem)
-    gate_load.start()
-    own_loads = []
-    for chunk in range(chunks):
-        own = pltpu.make_async_copy(
-            x_hbm.at[:, chunk * peers + amp, 0], yin.at[chunk, amp], own_sem.at[chunk]
-        )
-        own.start()
-        own_loads.append(own)
-
-    in_copies = []
-    for chunk in range(chunks):
-        copies = {}
-        for k in order:
-            peer = partner(amp, k)
-            copies[k] = pltpu.make_async_remote_copy(
-                src_ref=xs.at[chunk * peers + peer],
-                dst_ref=yin.at[chunk, amp],
-                send_sem=isend.at[chunk, k],
-                recv_sem=irecv.at[chunk, k],
-                device_id={"amp": peer},
-                device_id_type=MESH,
-            )
-        in_copies.append(copies)
+    far = list(range(3 * peers // 4, peers))
+    mid = list(range(peers // 2, 3 * peers // 4))
+    near = list(range(peers // 2 - 1, 0, -1))
+    groups = [far, mid, near]
 
     def tell(semaphore, axis, index, k):
         pl.semaphore_signal(
@@ -183,80 +158,127 @@
         )
 
     barrier = pltpu.get_barrier_semaphore()
-    if peers == 8 and sections == 4:
-        pair_at = amp // 2
-        inner_pair = (pair_at + 1) // 2 % 2
-        is_inner = inner_pair == 1
-        for k in (1, 2):
-            tell(barrier, "segment", seg, k)
-        for k in (1, 2, 3):
-            tell(barrier, "amp", amp, k)
+    line = peers == 8 and sections == 4
+    pair_at = amp // 2
+    inner_pair = (pair_at + 1) // 2 % 2
+    is_inner = inner_pair == 1
+    if line:
 
         @pl.when(is_inner)
         def _():
             tell(barrier, "amp", amp, 6)
             tell(barrier, "amp", amp, 7)
 
-        for load in loads:
-            load.wait()
-        pl.semaphore_wait(barrier, 5 + 2 * inner_pair)
+        for k in (3, 2, 1):
+            tell(barrier, "amp", amp, k)
+        for k in (1, 2):
+            tell(barrier, "segment", seg, k)
+    else:
+        for k in range(peers - 1, 0, -1):
+            tell(barrier, "amp", amp, k)
+        for k in range(1, sections):
+            tell(barrier, "segment", seg, k)
+
+    def load(chunk, k, semaphore):
+        m = chunk * peers + partner(amp, k)
+        pltpu.make_async_copy(x_hbm.at[:, m, 0], xs.at[chunk, k - 1], semaphore).start()
+
+    for g, group in enumerate(groups):
+        for k in group:
+            load(0, k, x_sem.at[g])
+    for chunk in range(1, chunks):
+        for group in groups:
+            for k in group:
+                load(chunk, k, x_sem.at[len(groups)])
+    gate_load = pltpu.make_async_copy(gates_hbm, gates.at[seg], gate_sem)
+    gate_load.start()
+    picks_load = pltpu.make_async_copy(picks_hbm, picks, small_sem.at[0])
+    picks_load.start()
+    targets_load = pltpu.make_async_copy(targets_hbm, targets, small_sem.at[1])
+    targets_load.start()
+    for chunk in range(chunks):
+        pltpu.make_async_copy(
+            x_hbm.at[:, chunk * peers + amp, 0], yin.at[chunk, amp], own_sem
+        ).start()
+
+    def send_in(chunk, k):
+        pltpu.make_async_remote_copy(
+            src_ref=xs.at[chunk, k - 1],
+            dst_ref=yin.at[chunk, amp],
+            send_sem=isend,
+            recv_sem=irecv.at[chunk],
+            device_id={"amp": partner(amp, k)},
+            device_id_type=MESH,
+        ).start()
+
+    def loaded(g):
+        slots = [k - 1 for k in groups[g]]
+        waits(xs.at[0, min(slots) : max(slots) + 1], x_sem.at[g])
+
+    with jax.named_scope("load0"):
+        loaded(0)
+    if line:
+        with jax.named_scope("barrier"):
+            pl.semaphore_wait(barrier, 5 + 2 * inner_pair)
 
         @pl.when(is_inner)
         def _():
             tell(entered.at[0], "amp", amp, 2)
             tell(entered.at[0], "amp", amp, 6)
-            in_copies[0][6].start()
-            in_copies[0][7].start()
+            send_in(0, 6)
+            send_in(0, 7)
 
         tell(entered.at[2], "segment", seg, 1)
-        pl.semaphore_wait(entered.at[0], 1)
+        loaded(1)
+        loaded(2)
+        with jax.named_scope("ent0"):
+            pl.semaphore_wait(entered.at[0], 1)
 
         @pl.when(is_inner)
         def _():
             tell(entered.at[1], "amp", amp, 2)
 
-        in_copies[0][4].start()
-        in_copies[0][5].start()
+        send_in(0, 4)
+        send_in(0, 5)
 
         @pl.when(jnp.logical_not(is_inner))
         def _():
-            pl.semaphore_wait(entered.at[1], 1)
-            in_copies[0][6].start()
-            in_copies[0][7].start()
-
-        for k in (3, 2, 1):
-            in_copies[0][k].start()
-        rest = in_copies[1:]
-        pl.semaphore_wait(entered.at[2], 1)
+            with jax.named_scope("ent1"):
+                pl.semaphore_wait(entered.at[1], 1)
+            send_in(0, 6)
+            send_in(0, 7)
+
+        for k in near:
+            send_in(0, k)
+        with jax.named_scope("ent2"):
+            pl.semaphore_wait(entered.at[2], 1)
     else:
-        for k in order:
-            tell(barrier, "amp", amp, k)
-        for k in range(1, sections):
-            tell(barrier, "segment", seg, k)
-        for load in loads:
-            load.wait()
         pl.semaphore_wait(barrier, peers - 1 + sections - 1)
-        rest = in_copies
-    for copies in rest:
-        for k in order:
-            copies[k].start()
-    in_copies = [list(copies.values()) for copies in in_copies]
-
+        loaded(1)
+        loaded(2)
+        for group in groups:
+            for k in group:
+                send_in(0, k)
     gate_load.wait()
-    gate_copies = []
     for k in range(1, sections):
-        copy = pltpu.make_async_remote_copy(
+        pltpu.make_async_remote_copy(
             src_ref=gates.at[seg],
             dst_ref=gates.at[seg],
-            send_sem=gsend.at[k],
-            recv_sem=grecv.at[k],
+            send_sem=gsend,
+            recv_sem=grecv,
             device_id={"segment": partner(seg, k)},
             device_id_type=MESH,
-        )
-        copy.start()
-        gate_copies.append(copy)
-    for copy in gate_copies:
-        copy.wait_recv()
+        ).start()
+    if chunks > 1:
+        waits(xs.at[1:], x_sem.at[len(groups)])
+    for chunk in range(1, chunks):
+        for group in groups:
+            for k in group:
+                send_in(chunk, k)
+    picks_load.wait()
+    targets_load.wait()
+    with jax.named_scope("gates"):
+        waits(gates.at[1:], grecv)
 
     rows_at = lax.broadcasted_iota(jnp.int32, (reg, reg), 0)
     columns_at = lax.broadcasted_iota(jnp.int32, (reg, reg), 1)
@@ -265,9 +287,9 @@
     def build(section, carry):
         low = high = None
         for b in range(blocks):
-            factors = row_factors(picks_ref, section, b, qubits, (reg, reg))
+            factors = row_factors(picks, section, b, qubits, (reg, reg))
             damped = gates[section, b] * factors
-            is_low = targets_ref[section, b] == 0
+            is_low = targets[section, b] == 0
             for_low = jnp.where(is_low, damped, identity)
             for_high = jnp.where(is_low, identity, damped)
             if b == 0:
@@ -279,7 +301,8 @@
         high_form[section] = left_form(high)
         return carry
 
-    lax.fori_loop(0, sections, build, 0)
+    with jax.named_scope("build"):
+        lax.fori_loop(0, sections, build, 0)
 
     inner = reg // peers
     partial[...] = jnp.zeros_like(partial)
@@ -304,56 +327,56 @@
                 yin[chunk, slab] = value
         partial[section + 1] = partial[section + 1] + total
 
-    out_copies = []
-    order_out = [5, 4, 7, 6, 3, 2, 1]
-    for chunk in range(chunks):
-        own_loads[chunk].wait()
-        for copy in in_copies[chunk]:
-            copy.wait_recv()
+    waits(ov.at[:, 0], own_sem)
+    order_out = mid + far + near
+
+    def run_chunk(chunk, carry):
+        with jax.named_scope("in"):
+            waits(xs.at[chunk], irecv.at[chunk])
         first = jnp.zeros((8, reg), jnp.float32)
         for slab in range(peers):
             first = first + fold_rows(yin[chunk, slab])
         partial[0] = partial[0] + first
 
-        def pair(i, carry, chunk=chunk):
+        def pair(i, inner_carry):
             apply_section(chunk, 2 * i, False)
             apply_section(chunk, 2 * i + 1, True)
-            return carry
-
-        lax.fori_loop(0, sections // 2, pair, 0)
-
-        if chunk == chunks - 1:
+            return inner_carry
+
+        with jax.named_scope("comp"):
+            lax.fori_loop(0, sections // 2, pair, 0)
+
+        @pl.when(chunk == chunks - 1)
+        def _():
             for s in range(sections + 1):
                 sums[amp, s : s + 1, :] = jnp.sum(partial[s], axis=0, keepdims=True)
-            sum_copies = []
-            for k in order:
-                copy = pltpu.make_async_remote_copy(
+            for k in range(peers - 1, 0, -1):
+                pltpu.make_async_remote_copy(
                     src_ref=sums.at[amp],
                     dst_ref=sums.at[amp],
-                    send_sem=ssend.at[k],
-                    recv_sem=srecv.at[k],
+                    send_sem=ssend,
+                    recv_sem=srecv,
                     device_id={"amp": partner(amp, k)},
                     device_id_type=MESH,
-                )
-                copy.start()
-                sum_copies.append(copy)
-        copies = []
+                ).start()
+
         for k in order_out:
+            g = [k in group for group in groups].index(True)
             peer = partner(amp, k)
-            copy = pltpu.make_async_remote_copy(
+            pltpu.make_async_remote_copy(
                 src_ref=yin.at[chunk, peer],
                 dst_ref=ov.at[chunk, amp],
-                send_sem=osend.at[chunk, k],
-                recv_sem=orecv.at[chunk, k],
+                send_sem=osend,
+                recv_sem=orecv.at[chunk, g],
                 device_id={"amp": peer},
                 device_id_type=MESH,
-            )
-            copy.start()
-            copies.append(copy)
-        out_copies.append(copies)
-
-    for copy in sum_copies:
-        copy.wait_recv()
+            ).start()
+        return carry
+
+    lax.fori_loop(0, chunks, run_chunk, 0)
+
+    with jax.named_scope("sums"):
+        waits(sums.at[1:], srecv)
     totals = []
     for s in range(sections + 1):
         total = sums[0, s : s + 1, :]
@@ -372,14 +395,30 @@
         m = chunk * peers + amp
         out_ref[pl.ds(m, reg, stride=middle), :] = yin[chunk, amp] * scale
     for chunk in range(chunks):
-        for at, k in reversed(list(enumerate(order_out))):
-            out_copies[chunk][at].wait_recv()
-            m = chunk * peers + partner(amp, k)
-            out_ref[pl.ds(m, reg, stride=middle), :] = ov[chunk, partner(amp, k)] * scale
-
-    for copies in in_copies + out_copies + [gate_copies, sum_copies]:
-        for copy in copies:
-            copy.wait_send()
+        for g in (2, 0, 1):
+            with jax.named_scope(f"out{chunk}_{g}"):
+                waits(xs.at[0, : len(groups[g])], orecv.at[chunk, g])
+            for k in groups[g]:
+                m = chunk * peers + partner(amp, k)
+                out_ref[pl.ds(m, reg, stride=middle), :] = ov[chunk, partner(amp, k)] * scale
+
+    with jax.named_scope("sendwait"):
+        waits(xs, isend)
+        waits(xs, osend)
+        waits(gates.at[1:], gsend)
+        waits(sums.at[1:], ssend)
+
+
+def store_kernel(pieces, out_vmem, logs_vmem, out_hbm, logs_hbm, sems):
+    rows = out_vmem.shape[0] // pieces
+    copies = [pltpu.make_async_copy(logs_vmem, logs_hbm, sems.at[pieces])]
+    for p in range(pieces):
+        at = pl.ds(p * rows, rows)
+        copies.append(pltpu.make_async_copy(out_vmem.at[at], out_hbm.at[at], sems.at[p]))
+    for copy in copies:
+        copy.start()
+    for copy in copies:
+        copy.wait()
 
 
 def step(states, gate_blocks, kraus_picks, block_targets):
@@ -395,6 +434,7 @@
         and gate_blocks.shape[0] == 1
         and middle % peers == 0
         and peers & (peers - 1) == 0
+        and peers >= 8
         and sections & (sections - 1) == 0
         and sections % 2 == 0
         and sections < 8
@@ -415,36 +455,34 @@
             pltpu.VMEM((reg * middle, reg), f32),
             pltpu.VMEM((1, sections), f32),
         ),
-        in_specs=[
-            pl.BlockSpec(memory_space=pl.ANY),
-            pl.BlockSpec(memory_space=pl.ANY),
-            pl.BlockSpec(memory_space=pltpu.SMEM),
-            pl.BlockSpec(memory_space=pltpu.SMEM),
-        ],
+        in_specs=[pl.BlockSpec(memory_space=pl.ANY)] * 4,
         out_specs=(
             pl.BlockSpec(memory_space=pltpu.VMEM),
             pl.BlockSpec(memory_space=pltpu.VMEM),
         ),
         scratch_shapes=[
-            pltpu.VMEM((middle, reg, reg), f32),
+            pltpu.VMEM((chunks, peers - 1, reg, reg), f32),
             pltpu.VMEM((chunks, peers, reg, reg), f32),
             pltpu.VMEM((chunks, peers, reg, reg), f32),
             pltpu.VMEM((sections, blocks, reg, reg), f32),
+            pltpu.SMEM((1, blocks, sections, qubits), jnp.int32),
+            pltpu.SMEM((sections, blocks), jnp.int32),
             pltpu.VMEM((sections, 2 * reg, 2 * reg), jnp.bfloat16),
             pltpu.VMEM((sections, reg, 2 * reg), jnp.bfloat16),
             pltpu.VMEM((sections + 1, 8, reg), f32),
             pltpu.VMEM((peers, 8, reg), f32),
-            dma((middle,)),
+            dma((4,)),
+            dma,
+            dma,
+            dma((2,)),
+            dma,
+            dma,
+            dma,
             dma((chunks,)),
             dma,
-            dma((sections,)),
-            dma((sections,)),
-            dma((chunks, peers)),
-            dma((chunks, peers)),
-            dma((chunks, peers)),
-            dma((chunks, peers)),
-            dma((peers,)),
-            dma((peers,)),
+            dma((chunks, 3)),
+            dma,
+            dma,
             pltpu.SemaphoreType.REGULAR((3,)),
         ],
         compiler_params=pltpu.CompilerParams(collective_id=0, has_side_effects=True),
@@ -454,6 +492,20 @@
         jnp.swapaxes(kraus_picks, 1, 2),
         block_targets,
     )
+    pieces = 4
+    out, logs = pl.pallas_call(
+        functools.partial(store_kernel, pieces),
+        out_shape=(
+            jax.ShapeDtypeStruct(out.shape, f32),
+            jax.ShapeDtypeStruct(logs.shape, f32),
+        ),
+        in_specs=[pl.BlockSpec(memory_space=pltpu.VMEM)] * 2,
+        out_specs=(pl.BlockSpec(memory_space=pl.ANY),) * 2,
+        scratch_shapes=[dma((pieces + 1,))],
+    )(
+        pltpu.with_memory_space_constraint(out, pltpu.VMEM),
+        pltpu.with_memory_space_constraint(logs, pltpu.VMEM),
+    )
     return out.reshape(1, amp_local), logs
 
 

time: 54.4 us -> 52.1 us (0.958)
  local copies, waits for them, and re-layouts: 1.48 us -> 0 us
    unnamed x2 -> x0, local copies, waits for them, and re-layouts: 1.48 us -> none
    pallas_call x1, Pallas kernels: 51.6 us -> 50.3 us  [step(): pl.pallas_call(kernel, out_shape=(pltpu.VMEM((reg * middle, reg), f32), p...]
    pallas_call x0 -> x1, Pallas kernels: none -> 1.01 us  [step(): pl.pallas_call(functools.partial(store_kernel, pieces), out_shape=(jax.Sh...]
where the time goes in v1:
time: 52.1 us; the launch traced here: 51.9 us
  Pallas kernels  51.3 us (98%)
  between operations  0.64 us (1%)
    pallas_call x1, Pallas kernels, step(): pl.pallas_call(kernel, out_shape=(pltpu.VMEM((reg * middle, reg), f32), p...  50.3 us

profile of v1, /device:TPU:9, one launch (start us, length us, event | category | flops | bytes accessed | tf_op | source)
XLA Modules:
  0.0 51.9 jit_solution(16695213002850296208)
XLA Ops:
  0.6 50.3 %shard_map.59 = (f32[2048,128]{1,0:T(8,128)S(1)}, f32[1,4]{1,0:T(1,128)S(1)}) custom-call(f32[128,16,1,128]{3,2,1,0:T(1,128)} %bitcast.4, f32[3,128,128]{2,1,0:T(8,128)} %bitcast.5, s32[1,3,4,7]{3,2,1,0:T(4,128)} %bitcast.6, s32[4,3]{1,0:T(4,128)} %targets_hbm.1), custom_call_target="tpu_custom_call" | custom-call | tf_op jit(solution)/shard_map/pallas_call | solution.py:452
  50.9 1.0 %shard_map.60 = (f32[2048,128]{1,0:T(8,128)}, f32[1,4]{1,0:T(1,128)}) custom-call(f32[2048,128]{1,0:T(8,128)S(1)} %get-tuple-element.6.out_vmem, f32[1,4]{1,0:T(1,128)S(1)} %get-tuple-element.7.logs_vmem), custom_call_target="tpu_custom_call" | custom-call | tf_op jit(solution)/shard_map/pallas_call | solution.py:496

commit v2 on v1

--- a/solution.py
+++ b/solution.py
@@ -140,7 +140,7 @@
     x_hbm, gates_hbm, picks_hbm, targets_hbm,
     out_ref, logs_ref,
     xs, yin, ov, gates, picks, targets, low_form, high_form, partial, sums,
-    x_sem, own_sem, gate_sem, small_sem, gsend, grecv, isend, irecv, osend, orecv, ssend, srecv,
+    x_sem, gate_sem, small_sem, sent, grecv, irecv, orecv, srecv,
     entered,
 ):
     seg = lax.axis_index("segment")
@@ -162,17 +162,22 @@
     pair_at = amp // 2
     inner_pair = (pair_at + 1) // 2 % 2
     is_inner = inner_pair == 1
+    late_inner = pair_at // 2 * inner_pair
+    early_inner = (1 - pair_at // 2) * inner_pair
     if line:
+
+        for k in (6, 7, 1):
+            tell(barrier, "amp", amp, k)
 
         @pl.when(is_inner)
         def _():
-            tell(barrier, "amp", amp, 6)
-            tell(barrier, "amp", amp, 7)
-
-        for k in (3, 2, 1):
-            tell(barrier, "amp", amp, k)
-        for k in (1, 2):
-            tell(barrier, "segment", seg, k)
+            for k in (2, 3, 4, 5):
+                tell(barrier, "amp", amp, k)
+
+        @pl.when(late_inner == 0)
+        def _():
+            for k in (1, 2):
+                tell(barrier, "segment", seg, k)
     else:
         for k in range(peers - 1, 0, -1):
             tell(barrier, "amp", amp, k)
@@ -183,13 +188,13 @@
         m = chunk * peers + partner(amp, k)
         pltpu.make_async_copy(x_hbm.at[:, m, 0], xs.at[chunk, k - 1], semaphore).start()
 
-    for g, group in enumerate(groups):
-        for k in group:
-            load(0, k, x_sem.at[g])
+    for k in far:
+        load(0, k, x_sem.at[0])
+    for k in mid + near:
+        load(0, k, x_sem.at[1])
     for chunk in range(1, chunks):
-        for group in groups:
-            for k in group:
-                load(chunk, k, x_sem.at[len(groups)])
+        for k in far + mid + near:
+            load(chunk, k, x_sem.at[2])
     gate_load = pltpu.make_async_copy(gates_hbm, gates.at[seg], gate_sem)
     gate_load.start()
     picks_load = pltpu.make_async_copy(picks_hbm, picks, small_sem.at[0])
@@ -198,64 +203,68 @@
     targets_load.start()
     for chunk in range(chunks):
         pltpu.make_async_copy(
-            x_hbm.at[:, chunk * peers + amp, 0], yin.at[chunk, amp], own_sem
+            x_hbm.at[:, chunk * peers + amp, 0], yin.at[chunk, amp], x_sem.at[1]
         ).start()
 
     def send_in(chunk, k):
         pltpu.make_async_remote_copy(
             src_ref=xs.at[chunk, k - 1],
             dst_ref=yin.at[chunk, amp],
-            send_sem=isend,
+            send_sem=sent,
             recv_sem=irecv.at[chunk],
             device_id={"amp": partner(amp, k)},
             device_id_type=MESH,
         ).start()
 
-    def loaded(g):
-        slots = [k - 1 for k in groups[g]]
-        waits(xs.at[0, min(slots) : max(slots) + 1], x_sem.at[g])
-
-    with jax.named_scope("load0"):
-        loaded(0)
+    def far_loaded():
+        waits(xs.at[0, : len(far)], x_sem.at[0])
+
+    def near_loaded():
+        waits(xs.at[0], x_sem.at[1])
+
     if line:
         with jax.named_scope("barrier"):
-            pl.semaphore_wait(barrier, 5 + 2 * inner_pair)
+            pl.semaphore_wait(barrier, 9 - 4 * inner_pair - 2 * late_inner)
+
+        @pl.when(late_inner == 0)
+        def _():
+            for k in (1, 2):
+                tell(entered.at[1], "segment", seg, k)
+
+        @pl.when(pair_at == peers // 2 - 1)
+        def _():
+            tell(entered.at[0], "amp", amp, 2)
+            tell(entered.at[0], "amp", amp, 4)
+
+        with jax.named_scope("load0"):
+            far_loaded()
+        send_in(0, 6)
+        send_in(0, 7)
+        near_loaded()
 
         @pl.when(is_inner)
         def _():
-            tell(entered.at[0], "amp", amp, 2)
-            tell(entered.at[0], "amp", amp, 6)
-            send_in(0, 6)
-            send_in(0, 7)
-
-        tell(entered.at[2], "segment", seg, 1)
-        loaded(1)
-        loaded(2)
-        with jax.named_scope("ent0"):
-            pl.semaphore_wait(entered.at[0], 1)
-
-        @pl.when(is_inner)
-        def _():
-            tell(entered.at[1], "amp", amp, 2)
-
-        send_in(0, 4)
-        send_in(0, 5)
-
-        @pl.when(jnp.logical_not(is_inner))
-        def _():
-            with jax.named_scope("ent1"):
-                pl.semaphore_wait(entered.at[1], 1)
-            send_in(0, 6)
-            send_in(0, 7)
-
-        for k in near:
+            with jax.named_scope("ent0"):
+                pl.semaphore_wait(entered.at[0], 1)
+
+        for k in [4, 5] + near:
             send_in(0, k)
-        with jax.named_scope("ent2"):
+        with jax.named_scope("ent1"):
+
+            @pl.when(late_inner == 0)
+            def _():
+                pl.semaphore_wait(entered.at[1], 2)
+                tell(entered.at[2], "segment", seg, 1)
+
             pl.semaphore_wait(entered.at[2], 1)
+
+            @pl.when(early_inner == 1)
+            def _():
+                tell(entered.at[2], "amp", amp, 6)
     else:
         pl.semaphore_wait(barrier, peers - 1 + sections - 1)
-        loaded(1)
-        loaded(2)
+        far_loaded()
+        near_loaded()
         for group in groups:
             for k in group:
                 send_in(0, k)
@@ -264,13 +273,13 @@
         pltpu.make_async_remote_copy(
             src_ref=gates.at[seg],
             dst_ref=gates.at[seg],
-            send_sem=gsend,
+            send_sem=sent,
             recv_sem=grecv,
             device_id={"segment": partner(seg, k)},
             device_id_type=MESH,
         ).start()
     if chunks > 1:
-        waits(xs.at[1:], x_sem.at[len(groups)])
+        waits(xs.at[1:], x_sem.at[2])
     for chunk in range(1, chunks):
         for group in groups:
             for k in group:
@@ -327,8 +336,10 @@
                 yin[chunk, slab] = value
         partial[section + 1] = partial[section + 1] + total
 
-    waits(ov.at[:, 0], own_sem)
     order_out = mid + far + near
+
+    def arrival(chunk, g):
+        return chunk + g * (chunk // (chunks - 1)) if chunks > 1 else g
 
     def run_chunk(chunk, carry):
         with jax.named_scope("in"):
@@ -354,7 +365,7 @@
                 pltpu.make_async_remote_copy(
                     src_ref=sums.at[amp],
                     dst_ref=sums.at[amp],
-                    send_sem=ssend,
+                    send_sem=sent,
                     recv_sem=srecv,
                     device_id={"amp": partner(amp, k)},
                     device_id_type=MESH,
@@ -366,8 +377,8 @@
             pltpu.make_async_remote_copy(
                 src_ref=yin.at[chunk, peer],
                 dst_ref=ov.at[chunk, amp],
-                send_sem=osend,
-                recv_sem=orecv.at[chunk, g],
+                send_sem=sent,
+                recv_sem=orecv.at[arrival(chunk, g)],
                 device_id={"amp": peer},
                 device_id_type=MESH,
             ).start()
@@ -394,19 +405,25 @@
     for chunk in range(chunks):
         m = chunk * peers + amp
         out_ref[pl.ds(m, reg, stride=middle), :] = yin[chunk, amp] * scale
-    for chunk in range(chunks):
-        for g in (2, 0, 1):
-            with jax.named_scope(f"out{chunk}_{g}"):
-                waits(xs.at[0, : len(groups[g])], orecv.at[chunk, g])
-            for k in groups[g]:
-                m = chunk * peers + partner(amp, k)
-                out_ref[pl.ds(m, reg, stride=middle), :] = ov[chunk, partner(amp, k)] * scale
+    def place(chunk, k):
+        m = chunk * peers + partner(amp, k)
+        out_ref[pl.ds(m, reg, stride=middle), :] = ov[chunk, partner(amp, k)] * scale
+
+    for chunk in range(chunks - 1):
+        waits(xs.at[0], orecv.at[chunk])
+        for k in order_out:
+            place(chunk, k)
+    for g in (2, 0, 1):
+        with jax.named_scope(f"out_{g}"):
+            waits(xs.at[0, : len(groups[g])], orecv.at[chunks - 1 + g])
+        for k in groups[g]:
+            place(chunks - 1, k)
 
     with jax.named_scope("sendwait"):
-        waits(xs, isend)
-        waits(xs, osend)
-        waits(gates.at[1:], gsend)
-        waits(sums.at[1:], ssend)
+        waits(xs, sent)
+        waits(xs, sent)
+        waits(gates.at[1:], sent)
+        waits(sums.at[1:], sent)
 
 
 def store_kernel(pieces, out_vmem, logs_vmem, out_hbm, logs_hbm, sems):
@@ -435,6 +452,7 @@
         and middle % peers == 0
         and peers & (peers - 1) == 0
         and peers >= 8
+        and middle == peers * (peers // 4)
         and sections & (sections - 1) == 0
         and sections % 2 == 0
         and sections < 8
@@ -471,17 +489,13 @@
             pltpu.VMEM((sections, reg, 2 * reg), jnp.bfloat16),
             pltpu.VMEM((sections + 1, 8, reg), f32),
             pltpu.VMEM((peers, 8, reg), f32),
-            dma((4,)),
-            dma,
+            dma((3,)),
             dma,
             dma((2,)),
             dma,
             dma,
-            dma,
             dma((chunks,)),
-            dma,
-            dma((chunks, 3)),
-            dma,
+            dma((chunks + 2,)),
             dma,
             pltpu.SemaphoreType.REGULAR((3,)),
         ],

time: 52.1 us -> 51.1 us (0.981)
  Pallas kernels: 51.3 us -> 50.3 us
    pallas_call x1, Pallas kernels: 50.3 us -> 49.3 us  [step(): pl.pallas_call(kernel, out_shape=(pltpu.VMEM((reg * middle, reg), f32), p...]
where the time goes in v2:
time: 51.1 us; the launch traced here: 50.9 us
  Pallas kernels  50.3 us (98%)
  between operations  0.64 us (1%)
    pallas_call x1, Pallas kernels, step(): pl.pallas_call(kernel, out_shape=(pltpu.VMEM((reg * middle, reg), f32), p...  49.3 us

profile of v2, /device:TPU:9, one launch (start us, length us, event | category | flops | bytes accessed | tf_op | source)
XLA Modules:
  0.0 50.9 jit_solution(3852850575553282388)
XLA Ops:
  0.6 49.3 %shard_map.59 = (f32[2048,128]{1,0:T(8,128)S(1)}, f32[1,4]{1,0:T(1,128)S(1)}) custom-call(f32[128,16,1,128]{3,2,1,0:T(1,128)} %bitcast.4, f32[3,128,128]{2,1,0:T(8,128)} %bitcast.5, s32[1,3,4,7]{3,2,1,0:T(4,128)} %bitcast.6, s32[4,3]{1,0:T(4,128)} %targets_hbm.1), custom_call_target="tpu_custom_call" | custom-call | tf_op jit(solution)/shard_map/pallas_call | solution.py:470
  49.9 1.0 %shard_map.60 = (f32[2048,128]{1,0:T(8,128)}, f32[1,4]{1,0:T(1,128)}) custom-call(f32[2048,128]{1,0:T(8,128)S(1)} %get-tuple-element.6.out_vmem, f32[1,4]{1,0:T(1,128)S(1)} %get-tuple-element.7.logs_vmem), custom_call_target="tpu_custom_call" | custom-call | tf_op jit(solution)/shard_map/pallas_call | solution.py:510

commit v3 on v2

--- a/solution.py
+++ b/solution.py
@@ -140,7 +140,7 @@
     x_hbm, gates_hbm, picks_hbm, targets_hbm,
     out_ref, logs_ref,
     xs, yin, ov, gates, picks, targets, low_form, high_form, partial, sums,
-    x_sem, gate_sem, small_sem, sent, grecv, irecv, orecv, srecv,
+    x_sem, small_sem, sent, grecv, irecv, orecv, srecv,
     entered,
 ):
     seg = lax.axis_index("segment")
@@ -157,6 +157,13 @@
             semaphore, inc=1, device_id={axis: partner(index, k)}, device_id_type=MESH
         )
 
+    def load(chunk, k, semaphore):
+        m = chunk * peers + partner(amp, k)
+        pltpu.make_async_copy(x_hbm.at[:, m, 0], xs.at[chunk, k - 1], semaphore).start()
+
+    for k in far:
+        load(0, k, x_sem.at[0])
+
     barrier = pltpu.get_barrier_semaphore()
     line = peers == 8 and sections == 4
     pair_at = amp // 2
@@ -184,19 +191,12 @@
         for k in range(1, sections):
             tell(barrier, "segment", seg, k)
 
-    def load(chunk, k, semaphore):
-        m = chunk * peers + partner(amp, k)
-        pltpu.make_async_copy(x_hbm.at[:, m, 0], xs.at[chunk, k - 1], semaphore).start()
-
-    for k in far:
-        load(0, k, x_sem.at[0])
     for k in mid + near:
         load(0, k, x_sem.at[1])
     for chunk in range(1, chunks):
         for k in far + mid + near:
-            load(chunk, k, x_sem.at[2])
-    gate_load = pltpu.make_async_copy(gates_hbm, gates.at[seg], gate_sem)
-    gate_load.start()
+            load(chunk, k, x_sem.at[1])
+    pltpu.make_async_copy(gates_hbm, gates.at[seg], x_sem.at[1]).start()
     picks_load = pltpu.make_async_copy(picks_hbm, picks, small_sem.at[0])
     picks_load.start()
     targets_load = pltpu.make_async_copy(targets_hbm, targets, small_sem.at[1])
@@ -219,8 +219,9 @@
     def far_loaded():
         waits(xs.at[0, : len(far)], x_sem.at[0])
 
-    def near_loaded():
-        waits(xs.at[0], x_sem.at[1])
+    def rest_loaded():
+        waits(xs, x_sem.at[1])
+        waits(gates.at[0], x_sem.at[1])
 
     if line:
         with jax.named_scope("barrier"):
@@ -240,7 +241,7 @@
             far_loaded()
         send_in(0, 6)
         send_in(0, 7)
-        near_loaded()
+        rest_loaded()
 
         @pl.when(is_inner)
         def _():
@@ -264,11 +265,10 @@
     else:
         pl.semaphore_wait(barrier, peers - 1 + sections - 1)
         far_loaded()
-        near_loaded()
+        rest_loaded()
         for group in groups:
             for k in group:
                 send_in(0, k)
-    gate_load.wait()
     for k in range(1, sections):
         pltpu.make_async_remote_copy(
             src_ref=gates.at[seg],
@@ -278,8 +278,6 @@
             device_id={"segment": partner(seg, k)},
             device_id_type=MESH,
         ).start()
-    if chunks > 1:
-        waits(xs.at[1:], x_sem.at[2])
     for chunk in range(1, chunks):
         for group in groups:
             for k in group:
@@ -314,6 +312,7 @@
         lax.fori_loop(0, sections, build, 0)
 
     inner = reg // peers
+    lanes = lax.broadcasted_iota(jnp.int32, (1, reg), 1)
     partial[...] = jnp.zeros_like(partial)
 
     def apply_section(chunk, section, swapped):
@@ -338,8 +337,9 @@
 
     order_out = mid + far + near
 
-    def arrival(chunk, g):
-        return chunk + g * (chunk // (chunks - 1)) if chunks > 1 else g
+    def arrival(chunk, k):
+        slot = max(k - peers // 2 + 1, 0)
+        return chunk + slot * (chunk // (chunks - 1))
 
     def run_chunk(chunk, carry):
         with jax.named_scope("in"):
@@ -359,8 +359,11 @@
 
         @pl.when(chunk == chunks - 1)
         def _():
+            row = jnp.zeros((1, reg), jnp.float32)
             for s in range(sections + 1):
-                sums[amp, s : s + 1, :] = jnp.sum(partial[s], axis=0, keepdims=True)
+                total = jnp.sum(jnp.sum(partial[s], axis=0, keepdims=True), axis=1, keepdims=True)
+                row = jnp.where(lanes == s, total, row)
+            sums[amp] = row
             for k in range(peers - 1, 0, -1):
                 pltpu.make_async_remote_copy(
                     src_ref=sums.at[amp],
@@ -372,13 +375,12 @@
                 ).start()
 
         for k in order_out:
-            g = [k in group for group in groups].index(True)
             peer = partner(amp, k)
             pltpu.make_async_remote_copy(
                 src_ref=yin.at[chunk, peer],
                 dst_ref=ov.at[chunk, amp],
                 send_sem=sent,
-                recv_sem=orecv.at[arrival(chunk, g)],
+                recv_sem=orecv.at[arrival(chunk, k)],
                 device_id={"amp": peer},
                 device_id_type=MESH,
             ).start()
@@ -388,13 +390,13 @@
 
     with jax.named_scope("sums"):
         waits(sums.at[1:], srecv)
-    totals = []
-    for s in range(sections + 1):
-        total = sums[0, s : s + 1, :]
-        for d in range(1, peers):
-            total = total + sums[d, s : s + 1, :]
-        totals.append(jnp.sum(total, axis=1, keepdims=True))
-    lanes = lax.broadcasted_iota(jnp.int32, (1, reg), 1)
+    row = sums[0]
+    for d in range(1, peers):
+        row = row + sums[d]
+    totals = [
+        jnp.sum(jnp.where(lanes == s, row, 0.0), axis=1, keepdims=True)
+        for s in range(sections + 1)
+    ]
     logs = jnp.zeros((1, reg), jnp.float32)
     for s in range(sections):
         logs = jnp.where(lanes == s, jnp.log(totals[s + 1] / totals[s]), logs)
@@ -405,19 +407,27 @@
     for chunk in range(chunks):
         m = chunk * peers + amp
         out_ref[pl.ds(m, reg, stride=middle), :] = yin[chunk, amp] * scale
-    def place(chunk, k):
-        m = chunk * peers + partner(amp, k)
-        out_ref[pl.ds(m, reg, stride=middle), :] = ov[chunk, partner(amp, k)] * scale
-
-    for chunk in range(chunks - 1):
+    def place(chunk, peer):
+        m = chunk * peers + peer
+        out_ref[pl.ds(m, reg, stride=middle), :] = ov[chunk, peer] * scale
+
+    last = chunks - 1
+    for chunk in range(last):
         waits(xs.at[0], orecv.at[chunk])
         for k in order_out:
-            place(chunk, k)
-    for g in (2, 0, 1):
-        with jax.named_scope(f"out_{g}"):
-            waits(xs.at[0, : len(groups[g])], orecv.at[chunks - 1 + g])
-        for k in groups[g]:
-            place(chunks - 1, k)
+            place(chunk, partner(amp, k))
+    with jax.named_scope("out_near"):
+        waits(xs.at[0, : len(near)], orecv.at[last])
+    for k in near:
+        place(last, partner(amp, k))
+    half = peers // 2
+    for at in range(half):
+        ahead = (at + half // 2) % half
+        slot = inner_pair * at + (1 - inner_pair) * ahead
+        peer = inner_pair * partner(amp, half + at) + (1 - inner_pair) * partner(amp, half + ahead)
+        with jax.named_scope(f"out_{at}"):
+            waits(xs.at[0, 0], orecv.at[last + 1 + slot])
+        place(last, peer)
 
     with jax.named_scope("sendwait"):
         waits(xs, sent)
@@ -453,6 +463,7 @@
         and peers & (peers - 1) == 0
         and peers >= 8
         and middle == peers * (peers // 4)
+        and middle > peers
         and sections & (sections - 1) == 0
         and sections % 2 == 0
         and sections < 8
@@ -488,14 +499,13 @@
             pltpu.VMEM((sections, 2 * reg, 2 * reg), jnp.bfloat16),
             pltpu.VMEM((sections, reg, 2 * reg), jnp.bfloat16),
             pltpu.VMEM((sections + 1, 8, reg), f32),
-            pltpu.VMEM((peers, 8, reg), f32),
-            dma((3,)),
-            dma,
+            pltpu.VMEM((peers, 1, reg), f32),
+            dma((2,)),
             dma((2,)),
             dma,
             dma,
             dma((chunks,)),
-            dma((chunks + 2,)),
+            dma((chunks + peers // 2,)),
             dma,
             pltpu.SemaphoreType.REGULAR((3,)),
         ],

time: 51.1 us -> 50.3 us (0.984)
  Pallas kernels: 50.3 us -> 49.5 us
    pallas_call x1, Pallas kernels: 49.3 us -> 48.5 us  [step(): pl.pallas_call(kernel, out_shape=(pltpu.VMEM((reg * middle, reg), f32), p...]
where the time goes in v3:
time: 50.3 us; the launch traced here: 50.1 us
  Pallas kernels  49.5 us (98%)
  between operations  0.64 us (1%)
    pallas_call x1, Pallas kernels, step(): pl.pallas_call(kernel, out_shape=(pltpu.VMEM((reg * middle, reg), f32), p...  48.5 us
    pallas_call x1, Pallas kernels, step(): pl.pallas_call(functools.partial(store_kernel, pieces), out_shape=(jax.Sh...  1.01 us

profile of v3, /device:TPU:9, one launch (start us, length us, event | category | flops | bytes accessed | tf_op | source)
XLA Modules:
  0.0 50.1 jit_solution(17674650645502472064)
XLA Ops:
  0.6 48.5 %shard_map.59 = (f32[2048,128]{1,0:T(8,128)S(1)}, f32[1,4]{1,0:T(1,128)S(1)}) custom-call(f32[128,16,1,128]{3,2,1,0:T(1,128)} %bitcast.4, f32[3,128,128]{2,1,0:T(8,128)} %bitcast.5, s32[1,3,4,7]{3,2,1,0:T(4,128)} %bitcast.6, s32[4,3]{1,0:T(4,128)} %targets_hbm.1), custom_call_target="tpu_custom_call" | custom-call | tf_op jit(solution)/shard_map/pallas_call | solution.py:481
  49.1 1.0 %shard_map.60 = (f32[2048,128]{1,0:T(8,128)}, f32[1,4]{1,0:T(1,128)}) custom-call(f32[2048,128]{1,0:T(8,128)S(1)} %get-tuple-element.6.out_vmem, f32[1,4]{1,0:T(1,128)S(1)} %get-tuple-element.7.logs_vmem), custom_call_target="tpu_custom_call" | custom-call | tf_op jit(solution)/shard_map/pallas_call | solution.py:520

commit v4 on v3

--- a/solution.py
+++ b/solution.py
@@ -157,12 +157,19 @@
             semaphore, inc=1, device_id={axis: partner(index, k)}, device_id_type=MESH
         )
 
-    def load(chunk, k, semaphore):
+    quarter = reg // 4
+    parts = [pl.ds(q * quarter, quarter) for q in range(4)]
+    first, others = parts[0], pl.ds(quarter, reg - quarter)
+
+    def load(chunk, k, semaphore, rows=pl.ds(0, reg)):
         m = chunk * peers + partner(amp, k)
-        pltpu.make_async_copy(x_hbm.at[:, m, 0], xs.at[chunk, k - 1], semaphore).start()
-
-    for k in far:
-        load(0, k, x_sem.at[0])
+        pltpu.make_async_copy(
+            x_hbm.at[rows, m, 0], xs.at[chunk, k - 1, rows], semaphore
+        ).start()
+
+    for q, rows in enumerate(parts):
+        for k in far:
+            load(0, k, x_sem.at[min(q, 1)], rows)
 
     barrier = pltpu.get_barrier_semaphore()
     line = peers == 8 and sections == 4
@@ -192,36 +199,36 @@
             tell(barrier, "segment", seg, k)
 
     for k in mid + near:
-        load(0, k, x_sem.at[1])
+        load(0, k, x_sem.at[2])
     for chunk in range(1, chunks):
         for k in far + mid + near:
-            load(chunk, k, x_sem.at[1])
-    pltpu.make_async_copy(gates_hbm, gates.at[seg], x_sem.at[1]).start()
-    picks_load = pltpu.make_async_copy(picks_hbm, picks, small_sem.at[0])
+            load(chunk, k, x_sem.at[2])
+    pltpu.make_async_copy(gates_hbm, gates.at[seg], x_sem.at[2]).start()
+    picks_load = pltpu.make_async_copy(picks_hbm, picks, small_sem)
     picks_load.start()
-    targets_load = pltpu.make_async_copy(targets_hbm, targets, small_sem.at[1])
+    targets_load = pltpu.make_async_copy(targets_hbm, targets, small_sem)
     targets_load.start()
     for chunk in range(chunks):
         pltpu.make_async_copy(
-            x_hbm.at[:, chunk * peers + amp, 0], yin.at[chunk, amp], x_sem.at[1]
+            x_hbm.at[:, chunk * peers + amp, 0], yin.at[chunk, amp], x_sem.at[2]
         ).start()
 
-    def send_in(chunk, k):
+    def send_in(chunk, k, rows=pl.ds(0, reg)):
         pltpu.make_async_remote_copy(
-            src_ref=xs.at[chunk, k - 1],
-            dst_ref=yin.at[chunk, amp],
+            src_ref=xs.at[chunk, k - 1, rows],
+            dst_ref=yin.at[chunk, amp, rows],
             send_sem=sent,
             recv_sem=irecv.at[chunk],
             device_id={"amp": partner(amp, k)},
             device_id_type=MESH,
         ).start()
 
-    def far_loaded():
-        waits(xs.at[0, : len(far)], x_sem.at[0])
+    def far_loaded(at):
+        waits(xs.at[0, : len(far), [first, others][at]], x_sem.at[at])
 
     def rest_loaded():
-        waits(xs, x_sem.at[1])
-        waits(gates.at[0], x_sem.at[1])
+        waits(xs, x_sem.at[2])
+        waits(gates.at[0], x_sem.at[2])
 
     if line:
         with jax.named_scope("barrier"):
@@ -237,10 +244,11 @@
             tell(entered.at[0], "amp", amp, 2)
             tell(entered.at[0], "amp", amp, 4)
 
-        with jax.named_scope("load0"):
-            far_loaded()
-        send_in(0, 6)
-        send_in(0, 7)
+        for at, rows in enumerate((first, others)):
+            with jax.named_scope("load0"):
+                far_loaded(at)
+            send_in(0, 6, rows)
+            send_in(0, 7, rows)
         rest_loaded()
 
         @pl.when(is_inner)
@@ -264,7 +272,8 @@
                 tell(entered.at[2], "amp", amp, 6)
     else:
         pl.semaphore_wait(barrier, peers - 1 + sections - 1)
-        far_loaded()
+        far_loaded(0)
+        far_loaded(1)
         rest_loaded()
         for group in groups:
             for k in group:
@@ -436,16 +445,15 @@
         waits(sums.at[1:], sent)
 
 
-def store_kernel(pieces, out_vmem, logs_vmem, out_hbm, logs_hbm, sems):
+def store_kernel(pieces, out_vmem, logs_vmem, out_hbm, logs_hbm, out_sem, logs_sem):
     rows = out_vmem.shape[0] // pieces
-    copies = [pltpu.make_async_copy(logs_vmem, logs_hbm, sems.at[pieces])]
     for p in range(pieces):
         at = pl.ds(p * rows, rows)
-        copies.append(pltpu.make_async_copy(out_vmem.at[at], out_hbm.at[at], sems.at[p]))
-    for copy in copies:
-        copy.start()
-    for copy in copies:
-        copy.wait()
+        pltpu.make_async_copy(out_vmem.at[at], out_hbm.at[at], out_sem).start()
+    logs_copy = pltpu.make_async_copy(logs_vmem, logs_hbm, logs_sem)
+    logs_copy.start()
+    pltpu.make_async_copy(out_vmem, out_hbm, out_sem).wait()
+    logs_copy.wait()
 
 
 def step(states, gate_blocks, kraus_picks, block_targets):
@@ -500,8 +508,8 @@
             pltpu.VMEM((sections, reg, 2 * reg), jnp.bfloat16),
             pltpu.VMEM((sections + 1, 8, reg), f32),
             pltpu.VMEM((peers, 1, reg), f32),
-            dma((2,)),
-            dma((2,)),
+            dma((3,)),
+            dma,
             dma,
             dma,
             dma((chunks,)),
@@ -516,7 +524,7 @@
         jnp.swapaxes(kraus_picks, 1, 2),
         block_targets,
     )
-    pieces = 4
+    pieces = 8
     out, logs = pl.pallas_call(
         functools.partial(store_kernel, pieces),
         out_shape=(
@@ -525,7 +533,7 @@
         ),
         in_specs=[pl.BlockSpec(memory_space=pltpu.VMEM)] * 2,
         out_specs=(pl.BlockSpec(memory_space=pl.ANY),) * 2,
-        scratch_shapes=[dma((pieces + 1,))],
+        scratch_shapes=[dma, dma],
     )(
         pltpu.with_memory_space_constraint(out, pltpu.VMEM),
         pltpu.with_memory_space_constraint(logs, pltpu.VMEM),

time: 50.3 us -> 50.2 us (level)
  no operation moved by 1% of the time
where the time goes in v4:
time: 50.2 us; the launch traced here: 50 us
  Pallas kernels  49.3 us (98%)
  between operations  0.64 us (1%)
    pallas_call x1, Pallas kernels, step(): pl.pallas_call(kernel, out_shape=(pltpu.VMEM((reg * middle, reg), f32), p...  48.4 us

profile of v4, /device:TPU:9, one launch (start us, length us, event | category | flops | bytes accessed | tf_op | source)
XLA Modules:
  0.0 50.0 jit_solution(17235844134013603383)
XLA Ops:
  0.6 48.4 %shard_map.59 = (f32[2048,128]{1,0:T(8,128)S(1)}, f32[1,4]{1,0:T(1,128)S(1)}) custom-call(f32[128,16,1,128]{3,2,1,0:T(1,128)} %bitcast.4, f32[3,128,128]{2,1,0:T(8,128)} %bitcast.5, s32[1,3,4,7]{3,2,1,0:T(4,128)} %bitcast.6, s32[4,3]{1,0:T(4,128)} %targets_hbm.1), custom_call_target="tpu_custom_call" | custom-call | tf_op jit(solution)/shard_map/pallas_call | solution.py:489
  49.0 1.0 %shard_map.60 = (f32[2048,128]{1,0:T(8,128)}, f32[1,4]{1,0:T(1,128)}) custom-call(f32[2048,128]{1,0:T(8,128)S(1)} %get-tuple-element.6.out_vmem, f32[1,4]{1,0:T(1,128)S(1)} %get-tuple-element.7.logs_vmem), custom_call_target="tpu_custom_call" | custom-call | tf_op jit(solution)/shard_map/pallas_call | solution.py:528

commit v5 on v4

--- a/solution.py
+++ b/solution.py
@@ -176,19 +176,25 @@
     pair_at = amp // 2
     inner_pair = (pair_at + 1) // 2 % 2
     is_inner = inner_pair == 1
-    late_inner = pair_at // 2 * inner_pair
-    early_inner = (1 - pair_at // 2) * inner_pair
+    first_core = amp % 2 * inner_pair
+    second_core = inner_pair - first_core
+    relays = second_core * (1 - pair_at // 2)
+    beside = 1 - inner_pair + relays
     if line:
 
-        for k in (6, 7, 1):
-            tell(barrier, "amp", amp, k)
+        tell(barrier, "amp", amp, 6)
+
+        @pl.when(second_core == 0)
+        def _():
+            tell(barrier, "amp", amp, 7)
+            tell(barrier, "amp", amp, 1)
 
         @pl.when(is_inner)
         def _():
             for k in (2, 3, 4, 5):
                 tell(barrier, "amp", amp, k)
 
-        @pl.when(late_inner == 0)
+        @pl.when(beside == 1)
         def _():
             for k in (1, 2):
                 tell(barrier, "segment", seg, k)
@@ -232,9 +238,11 @@
 
     if line:
         with jax.named_scope("barrier"):
-            pl.semaphore_wait(barrier, 9 - 4 * inner_pair - 2 * late_inner)
-
-        @pl.when(late_inner == 0)
+            pl.semaphore_wait(
+                barrier, 9 - 4 * inner_pair - 4 * first_core - 2 * (second_core - relays)
+            )
+
+        @pl.when(beside == 1)
         def _():
             for k in (1, 2):
                 tell(entered.at[1], "segment", seg, k)
@@ -248,28 +256,38 @@
             with jax.named_scope("load0"):
                 far_loaded(at)
             send_in(0, 6, rows)
-            send_in(0, 7, rows)
+
+            @pl.when(first_core == 0)
+            def _(rows=rows):
+                send_in(0, 7, rows)
+
         rest_loaded()
+        send_in(1, 6)
 
         @pl.when(is_inner)
         def _():
             with jax.named_scope("ent0"):
                 pl.semaphore_wait(entered.at[0], 1)
+
+        @pl.when(first_core == 1)
+        def _():
+            send_in(0, 7)
 
         for k in [4, 5] + near:
             send_in(0, k)
         with jax.named_scope("ent1"):
 
-            @pl.when(late_inner == 0)
+            @pl.when(beside == 1)
             def _():
                 pl.semaphore_wait(entered.at[1], 2)
                 tell(entered.at[2], "segment", seg, 1)
 
             pl.semaphore_wait(entered.at[2], 1)
 
-            @pl.when(early_inner == 1)
+            @pl.when(relays == 1)
             def _():
-                tell(entered.at[2], "amp", amp, 6)
+                for k in (6, 7, 1):
+                    tell(entered.at[2], "amp", amp, k)
     else:
         pl.semaphore_wait(barrier, peers - 1 + sections - 1)
         far_loaded(0)
@@ -288,8 +306,8 @@
             device_id_type=MESH,
         ).start()
     for chunk in range(1, chunks):
-        for group in groups:
-            for k in group:
+        for k in far + mid + near:
+            if not (line and chunk == 1 and k == 6):
                 send_in(chunk, k)
     picks_load.wait()
     targets_load.wait()

time: 50.2 us -> 50.1 us (level)
  no operation moved by 1% of the time
where the time goes in v5:
time: 50.1 us; the launch traced here: 50 us
  Pallas kernels  49.4 us (99%)
  between operations  0.64 us (1%)
    pallas_call x1, Pallas kernels, step(): pl.pallas_call(kernel, out_shape=(pltpu.VMEM((reg * middle, reg), f32), p...  48.4 us

profile of v5, /device:TPU:9, one launch (start us, length us, event | category | flops | bytes accessed | tf_op | source)
XLA Modules:
  0.0 50.0 jit_solution(15729410630757263996)
XLA Ops:
  0.6 48.4 %shard_map.59 = (f32[2048,128]{1,0:T(8,128)S(1)}, f32[1,4]{1,0:T(1,128)S(1)}) custom-call(f32[128,16,1,128]{3,2,1,0:T(1,128)} %bitcast.4, f32[3,128,128]{2,1,0:T(8,128)} %bitcast.5, s32[1,3,4,7]{3,2,1,0:T(4,128)} %bitcast.6, s32[4,3]{1,0:T(4,128)} %targets_hbm.1), custom_call_target="tpu_custom_call" | custom-call | tf_op jit(solution)/shard_map/pallas_call | solution.py:507
  49.0 1.0 %shard_map.60 = (f32[2048,128]{1,0:T(8,128)}, f32[1,4]{1,0:T(1,128)}) custom-call(f32[2048,128]{1,0:T(8,128)S(1)} %get-tuple-element.6.out_vmem, f32[1,4]{1,0:T(1,128)S(1)} %get-tuple-element.7.logs_vmem), custom_call_target="tpu_custom_call" | custom-call | tf_op jit(solution)/shard_map/pallas_call | solution.py:546

commit v6 on v5

--- a/solution.py
+++ b/solution.py
@@ -80,12 +80,16 @@
     return (amplitudes.reshape(traj_here, amp_local), log_weights)
 
 
+def quotient(index, divisor):
+    return index if divisor == 1 else lax.div(index, jnp.int32(divisor))
+
+
 def partner(index, k):
     result = index
     bit = 1
     while bit <= k:
         if k & bit:
-            result = result + bit * (1 - 2 * ((index // bit) % 2))
+            result = result + bit * (1 - 2 * lax.rem(quotient(index, bit), jnp.int32(2)))
         bit *= 2
     return result
 
@@ -140,7 +144,7 @@
     x_hbm, gates_hbm, picks_hbm, targets_hbm,
     out_ref, logs_ref,
     xs, yin, ov, gates, picks, targets, low_form, high_form, partial, sums,
-    x_sem, small_sem, sent, grecv, irecv, orecv, srecv,
+    x_sem, sent, grecv, irecv, orecv, srecv,
     entered,
 ):
     seg = lax.axis_index("segment")
@@ -173,12 +177,12 @@
 
     barrier = pltpu.get_barrier_semaphore()
     line = peers == 8 and sections == 4
-    pair_at = amp // 2
-    inner_pair = (pair_at + 1) // 2 % 2
+    pair_at = quotient(amp, 2)
+    inner_pair = lax.rem(quotient(pair_at + 1, 2), jnp.int32(2))
     is_inner = inner_pair == 1
-    first_core = amp % 2 * inner_pair
+    first_core = lax.rem(amp, jnp.int32(2)) * inner_pair
     second_core = inner_pair - first_core
-    relays = second_core * (1 - pair_at // 2)
+    relays = second_core * (1 - quotient(pair_at, 2))
     beside = 1 - inner_pair + relays
     if line:
 
@@ -210,9 +214,9 @@
         for k in far + mid + near:
             load(chunk, k, x_sem.at[2])
     pltpu.make_async_copy(gates_hbm, gates.at[seg], x_sem.at[2]).start()
-    picks_load = pltpu.make_async_copy(picks_hbm, picks, small_sem)
+    picks_load = pltpu.make_async_copy(picks_hbm, picks, x_sem.at[2])
     picks_load.start()
-    targets_load = pltpu.make_async_copy(targets_hbm, targets, small_sem)
+    targets_load = pltpu.make_async_copy(targets_hbm, targets, x_sem.at[2])
     targets_load.start()
     for chunk in range(chunks):
         pltpu.make_async_copy(
@@ -235,6 +239,8 @@
     def rest_loaded():
         waits(xs, x_sem.at[2])
         waits(gates.at[0], x_sem.at[2])
+        picks_load.wait()
+        targets_load.wait()
 
     if line:
         with jax.named_scope("barrier"):
@@ -309,8 +315,6 @@
         for k in far + mid + near:
             if not (line and chunk == 1 and k == 6):
                 send_in(chunk, k)
-    picks_load.wait()
-    targets_load.wait()
     with jax.named_scope("gates"):
         waits(gates.at[1:], grecv)
 
@@ -365,8 +369,10 @@
     order_out = mid + far + near
 
     def arrival(chunk, k):
-        slot = max(k - peers // 2 + 1, 0)
-        return chunk + slot * (chunk // (chunks - 1))
+        slot = 0
+        if k >= peers // 2:
+            slot = 1 + inner_pair * (1 + k % 2) if line else 1
+        return chunk + slot * quotient(chunk, chunks - 1)
 
     def run_chunk(chunk, carry):
         with jax.named_scope("in"):
@@ -447,14 +453,27 @@
         waits(xs.at[0, : len(near)], orecv.at[last])
     for k in near:
         place(last, partner(amp, k))
-    half = peers // 2
-    for at in range(half):
-        ahead = (at + half // 2) % half
-        slot = inner_pair * at + (1 - inner_pair) * ahead
-        peer = inner_pair * partner(amp, half + at) + (1 - inner_pair) * partner(amp, half + ahead)
-        with jax.named_scope(f"out_{at}"):
-            waits(xs.at[0, 0], orecv.at[last + 1 + slot])
-        place(last, peer)
+    if line:
+        late = [
+            inner_pair * partner(amp, 6 + at) + (1 - inner_pair) * partner(amp, 4 + at)
+            for at in range(2)
+        ]
+        soon = [
+            inner_pair * partner(amp, 4 + at) + (1 - inner_pair) * partner(amp, 6 + at)
+            for at in range(2)
+        ]
+        with jax.named_scope("out_soon"):
+            waits(xs.at[0, :2], orecv.at[last + 1])
+        for peer in soon:
+            place(last, peer)
+        for at in range(2):
+            with jax.named_scope(f"out_{at}"):
+                waits(xs.at[0, 0], orecv.at[last + 2 + at])
+            place(last, late[at])
+    else:
+        waits(xs.at[0, : peers // 2], orecv.at[last + 1])
+        for k in far + mid:
+            place(last, partner(amp, k))
 
     with jax.named_scope("sendwait"):
         waits(xs, sent)
@@ -529,9 +548,8 @@
             dma((3,)),
             dma,
             dma,
-            dma,
             dma((chunks,)),
-            dma((chunks + peers // 2,)),
+            dma((chunks + 3,)),
             dma,
             pltpu.SemaphoreType.REGULAR((3,)),
         ],

time: 50.1 us -> 50.1 us (level)
  no operation moved by 1% of the time
where the time goes in v6:
time: 50.1 us; the launch traced here: 50 us
  Pallas kernels  49.4 us (99%)
  between operations  0.64 us (1%)
    pallas_call x1, Pallas kernels, step(): pl.pallas_call(kernel, out_shape=(pltpu.VMEM((reg * middle, reg), f32), p...  48.4 us

profile of v6, /device:TPU:9, one launch (start us, length us, event | category | flops | bytes accessed | tf_op | source)
XLA Modules:
  0.0 50.0 jit_solution(13178320786268740011)
XLA Ops:
  0.6 48.4 %shard_map.59 = (f32[2048,128]{1,0:T(8,128)S(1)}, f32[1,4]{1,0:T(1,128)S(1)}) custom-call(f32[128,16,1,128]{3,2,1,0:T(1,128)} %bitcast.4, f32[3,128,128]{2,1,0:T(8,128)} %bitcast.5, s32[1,3,4,7]{3,2,1,0:T(4,128)} %bitcast.6, s32[4,3]{1,0:T(4,128)} %targets_hbm.1), custom_call_target="tpu_custom_call" | custom-call | tf_op jit(solution)/shard_map/pallas_call | solution.py:526
  49.0 1.0 %shard_map.60 = (f32[2048,128]{1,0:T(8,128)}, f32[1,4]{1,0:T(1,128)}) custom-call(f32[2048,128]{1,0:T(8,128)S(1)} %get-tuple-element.6.out_vmem, f32[1,4]{1,0:T(1,128)S(1)} %get-tuple-element.7.logs_vmem), custom_call_target="tpu_custom_call" | custom-call | tf_op jit(solution)/shard_map/pallas_call | solution.py:564

commit v7 on v6

--- a/solution.py
+++ b/solution.py
@@ -173,7 +173,7 @@
 
     for q, rows in enumerate(parts):
         for k in far:
-            load(0, k, x_sem.at[min(q, 1)], rows)
+            load(0, k, x_sem.at[0 if q == 0 and k == far[0] else 1], rows)
 
     barrier = pltpu.get_barrier_semaphore()
     line = peers == 8 and sections == 4
@@ -234,7 +234,11 @@
         ).start()
 
     def far_loaded(at):
-        waits(xs.at[0, : len(far), [first, others][at]], x_sem.at[at])
+        if at == 0:
+            waits(xs.at[0, 0, first], x_sem.at[0])
+        else:
+            waits(xs.at[0, : len(far) - 1], x_sem.at[1])
+            waits(xs.at[0, 0, others], x_sem.at[1])
 
     def rest_loaded():
         waits(xs, x_sem.at[2])
@@ -263,9 +267,9 @@
                 far_loaded(at)
             send_in(0, 6, rows)
 
-            @pl.when(first_core == 0)
-            def _(rows=rows):
-                send_in(0, 7, rows)
+        @pl.when(first_core == 0)
+        def _():
+            send_in(0, 7)
 
         rest_loaded()
         send_in(1, 6)
@@ -374,6 +378,16 @@
             slot = 1 + inner_pair * (1 + k % 2) if line else 1
         return chunk + slot * quotient(chunk, chunks - 1)
 
+    def send_sums(source, target, k, at):
+        pltpu.make_async_remote_copy(
+            src_ref=sums.at[source],
+            dst_ref=sums.at[target],
+            send_sem=sent,
+            recv_sem=srecv.at[at],
+            device_id={"amp": partner(amp, k)},
+            device_id_type=MESH,
+        ).start()
+
     def run_chunk(chunk, carry):
         with jax.named_scope("in"):
             waits(xs.at[chunk], irecv.at[chunk])
@@ -396,16 +410,9 @@
             for s in range(sections + 1):
                 total = jnp.sum(jnp.sum(partial[s], axis=0, keepdims=True), axis=1, keepdims=True)
                 row = jnp.where(lanes == s, total, row)
-            sums[amp] = row
-            for k in range(peers - 1, 0, -1):
-                pltpu.make_async_remote_copy(
-                    src_ref=sums.at[amp],
-                    dst_ref=sums.at[amp],
-                    send_sem=sent,
-                    recv_sem=srecv,
-                    device_id={"amp": partner(amp, k)},
-                    device_id_type=MESH,
-                ).start()
+            sums[pair_at] = row
+            for k in range(peers - 2, 0, -2):
+                send_sums(pair_at, pair_at, k, 0)
 
         for k in order_out:
             peer = partner(amp, k)
@@ -421,11 +428,17 @@
 
     lax.fori_loop(0, chunks, run_chunk, 0)
 
+    chips = peers // 2
     with jax.named_scope("sums"):
-        waits(sums.at[1:], srecv)
-    row = sums[0]
-    for d in range(1, peers):
-        row = row + sums[d]
+        waits(sums.at[1:chips], srecv.at[0])
+    part = sums[0]
+    for chip in range(1, chips):
+        part = part + sums[chip]
+    sums[chips] = part
+    send_sums(chips, chips + 1, 1, 1)
+    with jax.named_scope("join"):
+        waits(sums.at[0], srecv.at[1])
+    row = part + sums[chips + 1]
     totals = [
         jnp.sum(jnp.where(lanes == s, row, 0.0), axis=1, keepdims=True)
         for s in range(sections + 1)
@@ -479,7 +492,7 @@
         waits(xs, sent)
         waits(xs, sent)
         waits(gates.at[1:], sent)
-        waits(sums.at[1:], sent)
+        waits(sums.at[:chips], sent)
 
 
 def store_kernel(pieces, out_vmem, logs_vmem, out_hbm, logs_hbm, out_sem, logs_sem):
@@ -544,13 +557,13 @@
             pltpu.VMEM((sections, 2 * reg, 2 * reg), jnp.bfloat16),
             pltpu.VMEM((sections, reg, 2 * reg), jnp.bfloat16),
             pltpu.VMEM((sections + 1, 8, reg), f32),
-            pltpu.VMEM((peers, 1, reg), f32),
+            pltpu.VMEM((peers // 2 + 2, 1, reg), f32),
             dma((3,)),
             dma,
             dma,
             dma((chunks,)),
             dma((chunks + 3,)),
-            dma,
+            dma((2,)),
             pltpu.SemaphoreType.REGULAR((3,)),
         ],
         compiler_params=pltpu.CompilerParams(collective_id=0, has_side_effects=True),

time: 50.1 us -> 50.1 us (level)
  no operation moved by 1% of the time
where the time goes in v7:
time: 50.1 us; the launch traced here: 50 us
  Pallas kernels  49.3 us (98%)
  between operations  0.64 us (1%)
    pallas_call x1, Pallas kernels, step(): pl.pallas_call(kernel, out_shape=(pltpu.VMEM((reg * middle, reg), f32), p...  48.3 us

profile of v7, /device:TPU:9, one launch (start us, length us, event | category | flops | bytes accessed | tf_op | source)
XLA Modules:
  0.0 50.0 jit_solution(10660754227909745943)
XLA Ops:
  0.6 48.3 %shard_map.59 = (f32[2048,128]{1,0:T(8,128)S(1)}, f32[1,4]{1,0:T(1,128)S(1)}) custom-call(f32[128,16,1,128]{3,2,1,0:T(1,128)} %bitcast.4, f32[3,128,128]{2,1,0:T(8,128)} %bitcast.5, s32[1,3,4,7]{3,2,1,0:T(4,128)} %bitcast.6, s32[4,3]{1,0:T(4,128)} %targets_hbm.1), custom_call_target="tpu_custom_call" | custom-call | tf_op jit(solution)/shard_map/pallas_call | solution.py:539
  49.0 1.0 %shard_map.60 = (f32[2048,128]{1,0:T(8,128)}, f32[1,4]{1,0:T(1,128)}) custom-call(f32[2048,128]{1,0:T(8,128)S(1)} %get-tuple-element.6.out_vmem, f32[1,4]{1,0:T(1,128)S(1)} %get-tuple-element.7.logs_vmem), custom_call_target="tpu_custom_call" | custom-call | tf_op jit(solution)/shard_map/pallas_call | solution.py:577

commit v8 on v7

--- a/solution.py
+++ b/solution.py
@@ -373,10 +373,9 @@
     order_out = mid + far + near
 
     def arrival(chunk, k):
-        slot = 0
-        if k >= peers // 2:
-            slot = 1 + inner_pair * (1 + k % 2) if line else 1
-        return chunk + slot * quotient(chunk, chunks - 1)
+        if not line or k < peers // 2:
+            return 0
+        return quotient(chunk, chunks - 1) * inner_pair * (1 + k % 2)
 
     def send_sums(source, target, k, at):
         pltpu.make_async_remote_copy(
@@ -458,12 +457,12 @@
         out_ref[pl.ds(m, reg, stride=middle), :] = ov[chunk, peer] * scale
 
     last = chunks - 1
+    early = chunks * (peers - 1) - (2 if line else 0)
+    with jax.named_scope("early"):
+        waits(ov.at[:, :, : early * reg // (chunks * peers)], orecv.at[0])
     for chunk in range(last):
-        waits(xs.at[0], orecv.at[chunk])
         for k in order_out:
             place(chunk, partner(amp, k))
-    with jax.named_scope("out_near"):
-        waits(xs.at[0, : len(near)], orecv.at[last])
     for k in near:
         place(last, partner(amp, k))
     if line:
@@ -475,16 +474,13 @@
             inner_pair * partner(amp, 4 + at) + (1 - inner_pair) * partner(amp, 6 + at)
             for at in range(2)
         ]
-        with jax.named_scope("out_soon"):
-            waits(xs.at[0, :2], orecv.at[last + 1])
         for peer in soon:
             place(last, peer)
         for at in range(2):
             with jax.named_scope(f"out_{at}"):
-                waits(xs.at[0, 0], orecv.at[last + 2 + at])
+                waits(xs.at[0, 0], orecv.at[1 + at])
             place(last, late[at])
     else:
-        waits(xs.at[0, : peers // 2], orecv.at[last + 1])
         for k in far + mid:
             place(last, partner(amp, k))
 
@@ -562,7 +558,7 @@
             dma,
             dma,
             dma((chunks,)),
-            dma((chunks + 3,)),
+            dma((3,)),
             dma((2,)),
             pltpu.SemaphoreType.REGULAR((3,)),
         ],

time: 50.1 us -> 50.1 us (level)
  no operation moved by 1% of the time
where the time goes in v8:
time: 50.1 us; the launch traced here: 49.9 us
  Pallas kernels  49.3 us (98%)
  between operations  0.64 us (1%)
    pallas_call x1, Pallas kernels, step(): pl.pallas_call(kernel, out_shape=(pltpu.VMEM((reg * middle, reg), f32), p...  48.3 us

profile of v8, /device:TPU:9, one launch (start us, length us, event | category | flops | bytes accessed | tf_op | source)
XLA Modules:
  0.0 49.9 jit_solution(7206739227716291725)
XLA Ops:
  0.6 48.3 %shard_map.59 = (f32[2048,128]{1,0:T(8,128)S(1)}, f32[1,4]{1,0:T(1,128)S(1)}) custom-call(f32[128,16,1,128]{3,2,1,0:T(1,128)} %bitcast.4, f32[3,128,128]{2,1,0:T(8,128)} %bitcast.5, s32[1,3,4,7]{3,2,1,0:T(4,128)} %bitcast.6, s32[4,3]{1,0:T(4,128)} %targets_hbm.1), custom_call_target="tpu_custom_call" | custom-call | tf_op jit(solution)/shard_map/pallas_call | solution.py:535
  49.0 1.0 %shard_map.60 = (f32[2048,128]{1,0:T(8,128)}, f32[1,4]{1,0:T(1,128)}) custom-call(f32[2048,128]{1,0:T(8,128)S(1)} %get-tuple-element.6.out_vmem, f32[1,4]{1,0:T(1,128)S(1)} %get-tuple-element.7.logs_vmem), custom_call_target="tpu_custom_call" | custom-call | tf_op jit(solution)/shard_map/pallas_call | solution.py:573

commit v9 on v8

--- a/solution.py
+++ b/solution.py
@@ -161,9 +161,10 @@
             semaphore, inc=1, device_id={axis: partner(index, k)}, device_id_type=MESH
         )
 
-    quarter = reg // 4
-    parts = [pl.ds(q * quarter, quarter) for q in range(4)]
-    first, others = parts[0], pl.ds(quarter, reg - quarter)
+    eighth = reg // 8
+    edges = [0, 1, 3, 5, 8]
+    parts = [pl.ds(a * eighth, (b - a) * eighth) for a, b in zip(edges, edges[1:])]
+    first, others = parts[0], pl.ds(eighth, reg - eighth)
 
     def load(chunk, k, semaphore, rows=pl.ds(0, reg)):
         m = chunk * peers + partner(amp, k)

time: 50.1 us -> 50.1 us (level)
  no operation moved by 1% of the time
where the time goes in v9:
time: 50.1 us; the launch traced here: 49.9 us
  Pallas kernels  49.3 us (98%)
  between operations  0.64 us (1%)
    pallas_call x1, Pallas kernels, step(): pl.pallas_call(kernel, out_shape=(pltpu.VMEM((reg * middle, reg), f32), p...  48.3 us

profile of v9, /device:TPU:9, one launch (start us, length us, event | category | flops | bytes accessed | tf_op | source)
XLA Modules:
  0.0 49.9 jit_solution(11455400147686606933)
XLA Ops:
  0.6 48.3 %shard_map.59 = (f32[2048,128]{1,0:T(8,128)S(1)}, f32[1,4]{1,0:T(1,128)S(1)}) custom-call(f32[128,16,1,128]{3,2,1,0:T(1,128)} %bitcast.4, f32[3,128,128]{2,1,0:T(8,128)} %bitcast.5, s32[1,3,4,7]{3,2,1,0:T(4,128)} %bitcast.6, s32[4,3]{1,0:T(4,128)} %targets_hbm.1), custom_call_target="tpu_custom_call" | custom-call | tf_op jit(solution)/shard_map/pallas_call | solution.py:536
  49.0 1.0 %shard_map.60 = (f32[2048,128]{1,0:T(8,128)}, f32[1,4]{1,0:T(1,128)}) custom-call(f32[2048,128]{1,0:T(8,128)S(1)} %get-tuple-element.6.out_vmem, f32[1,4]{1,0:T(1,128)S(1)} %get-tuple-element.7.logs_vmem), custom_call_target="tpu_custom_call" | custom-call | tf_op jit(solution)/shard_map/pallas_call | solution.py:574

commit v10 on v9

--- a/solution.py
+++ b/solution.py
@@ -173,8 +173,10 @@
         ).start()
 
     for q, rows in enumerate(parts):
-        for k in far:
-            load(0, k, x_sem.at[0 if q == 0 and k == far[0] else 1], rows)
+        load(0, far[0], x_sem.at[min(q, 1)], rows)
+    for k in far[1:]:
+        for rows in parts[1:] + parts[:1]:
+            load(0, k, x_sem.at[3], rows)
 
     barrier = pltpu.get_barrier_semaphore()
     line = peers == 8 and sections == 4
@@ -238,7 +240,6 @@
         if at == 0:
             waits(xs.at[0, 0, first], x_sem.at[0])
         else:
-            waits(xs.at[0, : len(far) - 1], x_sem.at[1])
             waits(xs.at[0, 0, others], x_sem.at[1])
 
     def rest_loaded():
@@ -267,6 +268,7 @@
             with jax.named_scope("load0"):
                 far_loaded(at)
             send_in(0, 6, rows)
+        waits(xs.at[0, : len(far) - 1], x_sem.at[3])
 
         @pl.when(first_core == 0)
         def _():
@@ -303,6 +305,7 @@
         pl.semaphore_wait(barrier, peers - 1 + sections - 1)
         far_loaded(0)
         far_loaded(1)
+        waits(xs.at[0, : len(far) - 1], x_sem.at[3])
         rest_loaded()
         for group in groups:
             for k in group:
@@ -555,7 +558,7 @@
             pltpu.VMEM((sections, reg, 2 * reg), jnp.bfloat16),
             pltpu.VMEM((sections + 1, 8, reg), f32),
             pltpu.VMEM((peers // 2 + 2, 1, reg), f32),
-            dma((3,)),
+            dma((4,)),
             dma,
             dma,
             dma((chunks,)),

time: 50.1 us -> 50.1 us (level)
  no operation moved by 1% of the time
where the time goes in v10:
time: 50.1 us; the launch traced here: 49.9 us
  Pallas kernels  49.3 us (98%)
  between operations  0.64 us (1%)
    pallas_call x1, Pallas kernels, step(): pl.pallas_call(kernel, out_shape=(pltpu.VMEM((reg * middle, reg), f32), p...  48.3 us

profile of v10, /device:TPU:9, one launch (start us, length us, event | category | flops | bytes accessed | tf_op | source)
XLA Modules:
  0.0 49.9 jit_solution(4172861066017756517)
XLA Ops:
  0.6 48.3 %shard_map.59 = (f32[2048,128]{1,0:T(8,128)S(1)}, f32[1,4]{1,0:T(1,128)S(1)}) custom-call(f32[128,16,1,128]{3,2,1,0:T(1,128)} %bitcast.4, f32[3,128,128]{2,1,0:T(8,128)} %bitcast.5, s32[1,3,4,7]{3,2,1,0:T(4,128)} %bitcast.6, s32[4,3]{1,0:T(4,128)} %targets_hbm.1), custom_call_target="tpu_custom_call" | custom-call | tf_op jit(solution)/shard_map/pallas_call | solution.py:539
  49.0 1.0 %shard_map.60 = (f32[2048,128]{1,0:T(8,128)}, f32[1,4]{1,0:T(1,128)}) custom-call(f32[2048,128]{1,0:T(8,128)S(1)} %get-tuple-element.6.out_vmem, f32[1,4]{1,0:T(1,128)S(1)} %get-tuple-element.7.logs_vmem), custom_call_target="tpu_custom_call" | custom-call | tf_op jit(solution)/shard_map/pallas_call | solution.py:577
